TPU v7x, 32 devices: a whole 2x2x4 slice. The times are simulated.
32 devices in a mesh: rep: 8 (over z, core), shard: 4 (over y, x).
Axes of the slice: x: 2, y: 2, z: 4, core: 2. Of those that a mesh axis runs over, the one named last changes fastest.
Arguments:
- block_in: bfloat16 [4096, 2048], P(('rep', 'shard')), may hold values from -6 to 6
- segments: int32 [4096], P('rep'), may hold values from 0 to 15, never falling along the last dimension, each value on 1 to 512 neighbouring positions
- routes: int32 [4096, 8], P(('rep', 'shard')), may hold values from 0 to 31, all different within a row; in each aligned block of 128 rows (0 to 127, 128 to 255, ...) at most 64 rows name the same one
- attn_gain: float32 [2048], replicated, may hold values from 0.25 to 1.75
- query_key_value_weight: bfloat16 [2048, 5120], P('shard'), may hold values from -0.125 to 0.125
- q_gain: float32 [128], replicated, may hold values from 0.25 to 1.75
- k_gain: float32 [128], replicated, may hold values from 0.25 to 1.75
- w_out: bfloat16 [4096, 2048], P('shard'), may hold values from -1.5 to 1.5
- ffn_gain: float32 [2048], replicated, may hold values from 0.25 to 1.75
- router: bfloat16 [2048, 32], replicated, may hold values from -0.09375 to 0.09375
- expert_weights: bfloat16 [32, 3, 2048, 768], P(('rep', 'shard')), may hold values from -0.125 to 0.125
- cotangent: bfloat16 [4096, 2048], P(('rep', 'shard')), may hold values from -6 to 6
Outputs:
- block_out: bfloat16 [4096, 2048], P(('rep', 'shard'))
- grad_input: bfloat16 [4096, 2048], P(('rep', 'shard'))
- grad_attn_gain: float32 [2048], replicated
- grad_qkv: float32 [2048, 5120], P('shard')
- grad_q_gain: float32 [128], replicated
- grad_k_gain: float32 [128], replicated
- grad_out: float32 [4096, 2048], P('shard')
- grad_ffn_gain: float32 [2048], replicated
- grad_router: float32 [2048, 32], replicated
- grad_experts: float32 [32, 3, 2048, 768], P(('rep', 'shard'))
Inputs may be any that keep to these rules, and one draw needn't show every extreme that they name: `segments`: document numbers never fall along the tokens; a document has 1 to 512 tokens and one has exactly 512. `routes`: each row names 8 different experts; among the 128 rows of one device no expert is named more than 64 times, and in every draw some device names some expert exactly 64 times.
All inputs are finite; a program needn't handle non-finite values.
Results may differ from a plain program's by a relative error of at most 0.02.
Values may be sent and summed in bfloat16 or wider, within the bound.
A program may use at most 384 MiB of HBM per device.

v0:
```python
import jax
import jax.numpy as jnp
from jax import lax
from jax.sharding import PartitionSpec as P

QUERY_HEADS = 32
KEY_VALUE_HEADS = 4
HEAD_SIZE = 128


epsilon = 1e-06
rope_base = 1000000.0


def product(form, left, right):
    return jnp.einsum(form, left, right, preferred_element_type=jnp.float32)


def rms_scale(values):
    return lax.rsqrt(jnp.mean(values * values, axis=-1, keepdims=True) + epsilon)


def rms_back(values, scale, gain, upstream):
    scaled = upstream * gain
    cube = scale * scale * scale
    grad_values = scale * scaled - values * cube * jnp.mean(scaled * values, axis=-1, keepdims=True)
    grad_gain = jnp.sum((upstream * values * scale).reshape(-1, values.shape[-1]), axis=0)
    return (grad_values, grad_gain)


def rope_tables(positions):
    half = HEAD_SIZE // 2
    freq = rope_base ** (-jnp.arange(half).astype(jnp.float32) * 2.0 / HEAD_SIZE)
    angles = positions.astype(jnp.float32)[:, None] * freq[None, :]
    cosine = jnp.concatenate([jnp.cos(angles), jnp.cos(angles)], axis=-1)
    sine = jnp.concatenate([jnp.sin(angles), jnp.sin(angles)], axis=-1)
    return (cosine[:, None, :], sine[:, None, :])


def rotate(values):
    half = values.shape[-1] // 2
    return jnp.concatenate([-values[..., half:], values[..., :half]], axis=-1)


def rotate_back(values):
    half = values.shape[-1] // 2
    return jnp.concatenate([values[..., half:], -values[..., :half]], axis=-1)


def split_heads(query_key_value):
    token_rows = query_key_value.shape[0]
    q_raw = query_key_value[:, : QUERY_HEADS * HEAD_SIZE].reshape(
        token_rows, QUERY_HEADS, HEAD_SIZE
    )
    unrotated_key = query_key_value[
        :, QUERY_HEADS * HEAD_SIZE : (QUERY_HEADS + KEY_VALUE_HEADS) * HEAD_SIZE
    ].reshape(token_rows, KEY_VALUE_HEADS, HEAD_SIZE)
    projected_value = query_key_value[:, (QUERY_HEADS + KEY_VALUE_HEADS) * HEAD_SIZE :].reshape(
        token_rows, KEY_VALUE_HEADS, HEAD_SIZE
    )
    return (q_raw, unrotated_key, projected_value)


def norm_rope(raw, gain, cosine, sine):
    scale = rms_scale(raw)
    normed = raw * scale * gain
    return (scale, (normed * cosine + rotate(normed) * sine).astype(jnp.bfloat16))


def norm_rope_back(raw, scale, gain, cosine, sine, grad_rot):
    grad_normed = grad_rot * cosine + rotate_back(grad_rot * sine)
    return rms_back(raw, scale, gain, grad_normed)


def split_groups(values, groups):
    token_rows, heads, width = values.shape
    return values.reshape(token_rows, groups, heads // groups, width).transpose(1, 0, 2, 3)


def attend_forward(queries, keys, values, allowed):
    groups = keys.shape[1]
    token_rows = queries.shape[0]
    scale = queries.shape[2] ** (-0.5)

    def one_group(operands):
        q_part, k_part, v_part = operands
        scores = jnp.where(allowed[None], product("tpd,sd->pts", q_part, k_part) * scale, -1e30)
        highest = jnp.max(scores, axis=2, keepdims=True)
        lse = highest + jnp.log(jnp.sum(jnp.exp(scores - highest), axis=2, keepdims=True))
        probs = jnp.exp(scores - lse).astype(jnp.bfloat16)
        return (product("pts,sd->tpd", probs, v_part), lse[:, :, 0])

    outputs, lse = lax.map(
        one_group,
        (split_groups(queries, groups), keys.transpose(1, 0, 2), values.transpose(1, 0, 2)),
    )
    return (outputs.transpose(1, 0, 2, 3).reshape(token_rows, -1), lse)


def attend_backward(queries, keys, values, allowed, lse, attended, grad_attended):
    groups = keys.shape[1]
    token_rows, heads, width = queries.shape
    scale = width ** (-0.5)

    def one_group(operands):
        q_part, k_part, v_part, lse_part, out_part, grad_part = operands
        scores = jnp.where(allowed[None], product("tpd,sd->pts", q_part, k_part) * scale, -1e30)
        probs = jnp.exp(scores - lse_part[:, :, None])
        grad_v = product("pts,tpd->sd", probs.astype(jnp.bfloat16), grad_part)
        grad_p = product("tpd,sd->pts", grad_part, v_part)
        delta = jnp.sum(
            out_part.astype(jnp.float32) * grad_part.astype(jnp.float32), axis=2
        ).transpose(1, 0)
        grad_score = (probs * (grad_p - delta[:, :, None]) * scale).astype(jnp.bfloat16)
        return (
            product("pts,sd->tpd", grad_score, k_part),
            product("pts,tpd->sd", grad_score, q_part),
            grad_v,
        )

    shaped_out = split_groups(attended.reshape(token_rows, heads, width), groups)
    shaped_grad = split_groups(grad_attended.reshape(token_rows, heads, width), groups)
    grad_q, grad_k, grad_v = lax.map(
        one_group,
        (
            split_groups(queries, groups),
            keys.transpose(1, 0, 2),
            values.transpose(1, 0, 2),
            lse,
            shaped_out,
            shaped_grad,
        ),
    )
    return (
        grad_q.transpose(1, 0, 2, 3).reshape(token_rows, heads, width),
        grad_k.transpose(1, 0, 2),
        grad_v.transpose(1, 0, 2),
    )


def route_gates(normed, router, routes):
    logits = jnp.dot(normed, router, preferred_element_type=jnp.float32)
    weights = jax.nn.softmax(logits, axis=-1)
    chosen = (
        routes[:, :, None] == jnp.arange(router.shape[1], dtype=jnp.int32)[None, None, :]
    ).astype(jnp.float32)
    picked = jnp.sum(chosen * weights[:, None, :], axis=2)
    total = jnp.sum(picked, axis=1, keepdims=True)
    return (weights, chosen, picked, total, picked / total)


def route_gates_back(normed, router, weights, chosen, picked, total, grad_gates):
    grad_picked = grad_gates / total - jnp.sum(grad_gates * picked, axis=1, keepdims=True) / (
        total * total
    )
    grad_weights = jnp.sum(chosen * grad_picked[:, :, None], axis=1)
    grad_logits = weights * (grad_weights - jnp.sum(grad_weights * weights, axis=1, keepdims=True))
    grad_normed = jnp.dot(
        grad_logits, router.astype(jnp.float32).T, precision=lax.Precision.HIGHEST
    )
    grad_router = jnp.dot(
        normed.astype(jnp.float32).T, grad_logits, precision=lax.Precision.HIGHEST
    )
    return (grad_normed, grad_router)


def route_index(routes, experts, capacity):
    flat = routes.reshape(-1)
    onehot = (flat[:, None] == jnp.arange(experts, dtype=jnp.int32)[None, :]).astype(jnp.int32)
    before = jnp.cumsum(onehot, axis=0) - onehot
    return flat * capacity + jnp.sum(before * onehot, axis=1)


def dispatch(rows_per_route, index, experts, capacity):
    width = rows_per_route.shape[1]
    empty = jnp.zeros((experts * capacity, width), rows_per_route.dtype)
    return empty.at[index].set(rows_per_route).reshape(experts, capacity, width)


def collect(buffer, index):
    return buffer.reshape(-1, buffer.shape[-1])[index]


def expert_forward(inputs, weights):
    gate_pre = product("ecd,edf->ecf", inputs, weights[:, 0])
    up_pre = product("ecd,edf->ecf", inputs, weights[:, 1])
    hidden = (jax.nn.silu(gate_pre) * up_pre).astype(jnp.bfloat16)
    result = product("ecf,edf->ecd", hidden, weights[:, 2]).astype(jnp.bfloat16)
    return (gate_pre, up_pre, hidden, result)


def expert_backward(weights, gate_pre, up_pre, grad_result):
    grad_hidden = product("ecd,edf->ecf", grad_result, weights[:, 2])
    sig = jax.nn.sigmoid(gate_pre)
    grad_gate = (grad_hidden * up_pre * sig * (1.0 + gate_pre * (1.0 - sig))).astype(jnp.bfloat16)
    grad_up = (grad_hidden * gate_pre * sig).astype(jnp.bfloat16)
    grad_inputs = product("ecf,edf->ecd", grad_gate, weights[:, 0]) + product(
        "ecf,edf->ecd", grad_up, weights[:, 1]
    )
    return (grad_gate, grad_up, grad_inputs.astype(jnp.bfloat16))


def expert_weight_grads(inputs, hidden, grad_gate, grad_up, grad_result):
    return jnp.stack(
        [
            product("ecd,ecf->edf", inputs, grad_gate),
            product("ecd,ecf->edf", inputs, grad_up),
            product("ecd,ecf->edf", grad_result, hidden),
        ],
        axis=1,
    )


def body(
    block_in,
    segments,
    routes,
    attn_gain,
    query_key_value_weight,
    q_gain,
    k_gain,
    w_out,
    ffn_gain,
    router,
    expert_weights,
    cotangent,
):
    tok = block_in.shape[0]
    width = block_in.shape[1]
    top = routes.shape[1]
    rep_count = lax.axis_size("rep")
    shard_count = lax.axis_size("shard")
    experts = expert_weights.shape[0] * rep_count * shard_count
    capacity = tok * top * 2 // experts
    shard_pos = lax.axis_index("shard")
    qkv_whole, out_whole = (
        lax.all_gather(query_key_value_weight, "shard", axis=0, tiled=True),
        lax.all_gather(w_out, "shard", axis=0, tiled=True),
    )
    inputs = block_in.astype(jnp.float32)
    scale_one = rms_scale(inputs)
    normed_one = (inputs * scale_one * attn_gain).astype(jnp.bfloat16)
    query_key_value = jnp.dot(normed_one, qkv_whole, preferred_element_type=jnp.float32)
    q_raw, unrotated_key, projected_value = split_heads(query_key_value)
    positions = shard_pos * tok + jnp.arange(tok, dtype=jnp.int32)
    cosine, sine = rope_tables(positions)
    q_scale, q_rot = norm_rope(q_raw, q_gain, cosine, sine)
    k_scale, k_rot = norm_rope(unrotated_key, k_gain, cosine, sine)
    keys_all, values_all = (
        lax.all_gather(k_rot, "shard", axis=0, tiled=True),
        lax.all_gather(projected_value.astype(jnp.bfloat16), "shard", axis=0, tiled=True),
    )
    query_seg = lax.dynamic_slice_in_dim(segments, shard_pos * tok, tok)
    key_pos = jnp.arange(segments.shape[0], dtype=jnp.int32)
    allowed = (query_seg[:, None] == segments[None, :]) & (key_pos[None, :] <= positions[:, None])
    attended_f, lse = attend_forward(q_rot, keys_all, values_all, allowed)
    attended = attended_f.astype(jnp.bfloat16)
    middle = inputs + jnp.dot(attended, out_whole, preferred_element_type=jnp.float32)
    scale_two = rms_scale(middle)
    normed_two = (middle * scale_two * ffn_gain).astype(jnp.bfloat16)
    weights, chosen, picked, total, gates = route_gates(normed_two, router, routes)
    index = route_index(routes, experts, capacity)
    upstream = cotangent.astype(jnp.float32)
    grad_rows = (
        (gates[:, :, None] * upstream[:, None, :]).astype(jnp.bfloat16).reshape(tok * top, width)
    )
    paired = jnp.concatenate([jnp.repeat(normed_two, top, axis=0), grad_rows], axis=1)
    buffer = dispatch(paired, index, experts, capacity)
    received = lax.all_to_all(buffer, ("rep", "shard"), split_axis=0, concat_axis=1, tiled=True)
    token_rows = received[:, :, :width]
    grads = received[:, :, width:]
    gate_pre, up_pre, hidden, result = expert_forward(token_rows, expert_weights)
    grad_gate, grad_up, grad_inner = expert_backward(expert_weights, gate_pre, up_pre, grads)
    grad_experts = expert_weight_grads(token_rows, hidden, grad_gate, grad_up, grads)
    outgoing = jnp.concatenate([result, grad_inner], axis=2)
    returned = lax.all_to_all(outgoing, ("rep", "shard"), split_axis=1, concat_axis=0, tiled=True)
    fetched = collect(returned, index).reshape(tok, top, 2 * width)
    expert_rows = fetched[:, :, :width].astype(jnp.float32)
    grad_from_experts = jnp.sum(fetched[:, :, width:].astype(jnp.float32), axis=1)
    block_out = (middle + jnp.sum(gates[:, :, None] * expert_rows, axis=1)).astype(jnp.bfloat16)
    grad_gates = jnp.sum(expert_rows * upstream[:, None, :], axis=2)
    grad_from_router, grad_router = route_gates_back(
        normed_two, router, weights, chosen, picked, total, grad_gates
    )
    grad_norm_two, grad_ffn_gain = rms_back(
        middle, scale_two, ffn_gain, grad_from_experts + grad_from_router
    )
    grad_middle = upstream + grad_norm_two
    grad_middle_b = grad_middle.astype(jnp.bfloat16)
    columns = attended
    grad_out = lax.psum_scatter(
        lax.dot_general(
            columns, grad_middle_b, (((0,), (0,)), ((), ())), preferred_element_type=jnp.float32
        ).astype(jnp.bfloat16),
        "shard",
        scatter_dimension=0,
        tiled=True,
    ).astype(jnp.float32)
    grad_attended = jnp.dot(grad_middle_b, out_whole.T, preferred_element_type=jnp.float32).astype(
        jnp.bfloat16
    )
    grad_q_rot, grad_k_all, grad_v_all = attend_backward(
        q_rot, keys_all, values_all, allowed, lse, attended, grad_attended
    )
    grad_k_rot, grad_v = (
        lax.psum_scatter(
            grad_k_all.astype(jnp.bfloat16), "shard", scatter_dimension=0, tiled=True
        ).astype(jnp.float32),
        lax.psum_scatter(
            grad_v_all.astype(jnp.bfloat16), "shard", scatter_dimension=0, tiled=True
        ).astype(jnp.float32),
    )
    grad_q_raw, grad_q_gain = norm_rope_back(q_raw, q_scale, q_gain, cosine, sine, grad_q_rot)
    grad_k_raw, grad_k_gain = norm_rope_back(
        unrotated_key, k_scale, k_gain, cosine, sine, grad_k_rot
    )
    grad_qkv_b = jnp.concatenate(
        [grad_q_raw.reshape(tok, -1), grad_k_raw.reshape(tok, -1), grad_v.reshape(tok, -1)], axis=1
    ).astype(jnp.bfloat16)
    columns = normed_one
    grad_qkv = lax.psum_scatter(
        lax.dot_general(
            columns, grad_qkv_b, (((0,), (0,)), ((), ())), preferred_element_type=jnp.float32
        ).astype(jnp.bfloat16),
        "shard",
        scatter_dimension=0,
        tiled=True,
    ).astype(jnp.float32)
    grad_norm_one = jnp.dot(grad_qkv_b, qkv_whole.T, preferred_element_type=jnp.float32)
    grad_inputs, grad_attn_gain = rms_back(inputs, scale_one, attn_gain, grad_norm_one)
    grad_input = (grad_middle + grad_inputs).astype(jnp.bfloat16)
    grad_attn_gain, grad_q_gain, grad_k_gain, grad_ffn_gain, grad_router = lax.psum(
        (grad_attn_gain, grad_q_gain, grad_k_gain, grad_ffn_gain, grad_router), ("rep", "shard")
    )
    grad_qkv, grad_out = (
        lax.psum(grad_qkv.astype(jnp.bfloat16), "rep").astype(jnp.float32),
        lax.psum(grad_out.astype(jnp.bfloat16), "rep").astype(jnp.float32),
    )
    return (
        block_out,
        grad_input,
        grad_attn_gain,
        grad_qkv,
        grad_q_gain,
        grad_k_gain,
        grad_out,
        grad_ffn_gain,
        grad_router,
        grad_experts,
    )


def solution(mesh):
    placed = (
        P(("rep", "shard"), None),
        P("rep"),
        P(("rep", "shard"), None),
        P(),
        P("shard", None),
        P(),
        P(),
        P("shard", None),
        P(),
        P(),
        P(("rep", "shard"), None, None, None),
        P(("rep", "shard"), None),
    )
    return jax.shard_map(
        body,
        mesh=mesh,
        in_specs=placed,
        out_specs=(
            P(("rep", "shard"), None),
            P(("rep", "shard"), None),
            P(),
            P("shard", None),
            P(),
            P(),
            P("shard", None),
            P(),
            P(),
            P(("rep", "shard"), None, None, None),
        ),
        check_vma=False,
    )
```

profile of v0, /device:TPU:0, one launch (start us, length us, event | category | flops | bytes accessed | tf_op | source)
XLA Modules:
  0.0 2359.0 jit_solution(10408665407152502954)
XLA Ops:
  10.6 9.0 reduce-window.6
  22.0 183.6 %all-gather.3.cloned.1.call-done = bf16[2048,5120]{1,0:T(8,128)(2,1)} async-done(((bf16[512,5120]{1,0:T(8,128)(2,1)}), bf16[2048,5120]{1,0:T(8,128)(2,1)}) %all-gather.3.cloned.1.call-update) | async-done | bytes 20971536 | tf_op jit(solution)/shard_map/all_gather | solution.py:237
  205.7 8.6 fusion.115
  234.9 16.1 all_gather.14
  251.9 15.0 all_gather.13
  270.4 15.6 while.30
  286.1 87.2 %all-gather.5.cloned.1.call-done = bf16[4096,2048]{1,0:T(8,128)(2,1)} async-done(((bf16[1024,2048]{1,0:T(8,128)(2,1)}), bf16[4096,2048]{1,0:T(8,128)(2,1)}) %all-gather.5.cloned.1.call-update) | async-done | bytes 16777232 | tf_op jit(solution)/shard_map/all_gather | solution.py:238
  373.3 8.2 multiply_reduce_fusion.3
  389.7 8.0 pad_maximum_fusion.2
  397.7 22.8 scatter_custom_fusion
  420.5 368.8 %all_to_all.21 = bf16[32,64,4096]{2,1,0:T(8,128)(2,1)S(1)} all-to-all(bf16[32,64,4096]{2,1,0:T(8,128)(2,1)} %bitcast.378), channel_id=1, replica_groups=mesh['rep'=8,'shard'=4] {'rep','shard'}, dimensions={0} | all-to-all | bytes 33554432 | tf_op jit(solution)/shard_map/all_to_all | solution.py:269
  789.4 8.5 fusion.52
  797.9 8.5 fusion.56
  806.4 19.2 multiply_convert_fusion.2
  825.6 11.6 fusion.64
  837.2 9.5 convert_bitcast_fusion
  846.7 13.3 fusion.47
  860.0 10.6 pad_maximum_fusion.1
  870.6 72.3 %copy.313 = bf16[1,2048,4096]{2,0,1:T(2,128)(2,1)} copy(bf16[1,2048,4096]{1,2,0:T(8,128)(2,1)} %pad_maximum_fusion.1) | data formatting | bytes 33554432 | tf_op jit(solution)/shard_map/concatenate | solution.py:275
  943.4 102.5 %reduce.2 = bf16[2048,4096]{1,0:T(8,128)(2,1)} reduce(bf16[2048,1,4096]{2,1,0:T(2,128)(2,1)} %bitcast.376, bf16[]{:T(256)} %broadcast.324), dimensions={1}, to_apply=%bitcast.269.reduce_sub_computation | reduce | bytes 33554432
  1045.9 27.8 %reshape.465 = bf16[32,2,131072]{2,1,0:T(2,128)(2,1)} reshape(bf16[2048,4096]{1,0:T(8,128)(2,1)} %reduce.2) | data formatting | bytes 33554432
  1073.7 4.0 all-to-all-start.1
  1077.8 382.4 %all-to-all-done.1 = bf16[32,2,131072]{2,1,0:T(2,128)(2,1)} async-done(((bf16[32,2,131072]{2,1,0:T(2,128)(2,1)}), bf16[32,2,131072]{2,1,0:T(2,128)(2,1)}, u32[]{:S(2)}, u32[]{:S(2)}) %all-to-all-start.1) | async-done | bytes 16777248 | tf_op jit(solution)/shard_map/all_to_all | solution.py:276
  1460.2 31.8 %reshape.466 = bf16[2048,1,4096]{2,1,0:T(2,128)(2,1)} reshape(bf16[32,2,131072]{2,1,0:T(2,128)(2,1)} %all-to-all-done.1) | data formatting | bytes 33554432
  1492.0 30.2 %copy.380 = bf16[1,2048,4096]{2,1,0:T(8,128)(2,1)} copy(bf16[1,2048,4096]{2,0,1:T(2,128)(2,1)} %bitcast.377) | data formatting | bytes 33554432
  1522.2 23.1 gather_fusion
  1545.4 10.9 fusion.46
  1560.9 11.8 fusion.89
  1574.4 47.7 %while.31 = (s32[]{:T(128)}, f32[4,128,8,128]{1,3,2,0:T(8,128)}, bf16[4,512,128]{2,1,0:T(8,128)(2,1)}, bf16[4,512,128]{2,1,0:T(8,128)(2,1)}, bf16[4,512,128]{2,1...) while((s32[]{:T(128)}, f32[4,128,8,128]{1,3,2,0:T(8,128)}, ...), condition=%wide.region_25.26_spmd.clone.clone, body=%wide.region_23.25_spmd.clone.sunk.clone | while | flops 676002816 | bytes 22049016 | solution.py:123
  1622.7 11.8 convolution_convert_fusion.1
  1654.3 8.1 fusion.74
  1664.9 6.1 reduce-scatter.7.cloned.1.call-done
  1672.3 10.4 convolution_convert_fusion
  1685.8 12.1 fusion.57
  1698.0 129.7 %reduce-scatter.11.cloned.1.call-done = bf16[1024,2048]{1,0:T(8,128)(2,1)} async-done(((bf16[4096,2048]{1,0:T(8,128)(2,1)}), bf16[1024,2048]{1,0:T(8,128)(2,1)}) %reduce-scatter.11.cloned.1.call-update) | async-done | bytes 4194320 | tf_op jit(solution)/shard_map/reduce_scatter | solution.py:291
  1827.7 190.7 %reduce-scatter.9.cloned.1.call-done = bf16[512,5120]{1,0:T(8,128)(2,1)} async-done(((bf16[2048,5120]{1,0:T(8,128)(2,1)}), bf16[512,5120]{1,0:T(8,128)(2,1)}) %reduce-scatter.9.cloned.1.call-update) | async-done | bytes 5242896 | tf_op jit(solution)/shard_map/reduce_scatter | solution.py:321
  2018.5 10.6 fusion.58
  2029.2 9.7 fusion.59
  2038.9 7.0 pad_maximum_fusion
  2045.9 4.2 copy.329
  2050.1 4.0 copy.330
  2055.2 3.6 fusion.82
  2058.8 12.1 fusion.99
  2072.2 41.1 %all-reduce = (f32[2048]{0:T(1024)}, f32[128]{0:T(128)}, f32[128]{0:T(128)}, f32[2048]{0:T(1024)}) all-reduce(f32[2048]{0:T(1024)S(1)} %get-tuple-element.378, f32[128]{0:T(128)S(1)} %fusion.82, f32[128]{0:T(128)S(1)} %get-tuple-element.380, f32[2048]{0:T(1024)S(1)} %get-tuple-element.376), channel_id=1, replica_groups=mesh['rep'=8,'shard'=4] {'rep','shard'}, use_global_device_ids=true, to_apply=%region_32.33 | all-reduce | flops 4352 | bytes 34816 | tf_op jit(solution)/shard_map/psum | solution.py:332
  2113.3 104.0 %all-reduce.7.cloned.1.call-done = (bf16[512,5120]{1,0:T(8,128)(2,1)}, bf16[1024,2048]{1,0:T(8,128)(2,1)}) async-done(((bf16[512,5120]{1,0:T(8,128)(2,1)}, bf16[1024,2048]{1,0:T(8,128)(2,1)}), (bf16[512,5120]{1,0:T(8,128)(2,1)}, bf16[1024,2048]{1,0:T(8,128)(2,1)})) %all-reduce.7.cloned.1.call-update) | async-done | bytes 9437200 | tf_op jit(solution)/shard_map/psum | solution.py:336
  2217.3 8.1 convert_element_type.189
  2225.3 4.4 convert_element_type.191
  2229.8 120.2 %all-reduce.5.cloned.1.call-done = f32[2048,32]{0,1:T(8,128)} async-done(((f32[2048,32]{0,1:T(8,128)}), f32[2048,32]{0,1:T(8,128)}) %all-reduce.5.cloned.1.call-update) | async-done | bytes 262160 | tf_op jit(solution)/shard_map/psum | solution.py:332
  (407 shorter events, 139.2 us)
Async XLA Ops:
  7.2 378.4 %copy-start = (bf16[2048,32]{0,1:T(8,128)(2,1)S(1)}, bf16[2048,32]{0,1:T(8,128)(2,1)}, u32[]{:S(2)}) copy-start(bf16[2048,32]{0,1:T(8,128)(2,1)} %param.25) | copy-start | bytes 393220
  7.2 198.5 %all-gather.3.cloned.1.call-start = ((), (), s32[]{:S(2)}) async-start(), calls=%async_computation.6 | async-start | bytes 26214400 | tf_op jit(solution)/shard_map/all_gather | solution.py:237
  8.0 12.3 copy-start.61
  8.0 365.3 %all-gather.5.cloned.1.call-start = ((), (), s32[]{:S(2)}) async-start(), calls=%async_computation.7 | async-start | bytes 20971520 | tf_op jit(solution)/shard_map/all_gather | solution.py:238
  8.7 12.0 copy-start.15
  8.7 197.0 %copy-start.52 = (f32[2048]{0:T(1024)S(1)}, f32[2048]{0:T(1024)}, u32[]{:S(2)}) copy-start(f32[2048]{0:T(1024)} %param.19) | copy-start | bytes 24580
  9.3 205.0 %copy-start.36 = (f32[128,128]{0,1:T(8,128)}, f32[128,128]{0,1:T(8,128)S(1)}, u32[]{:S(2)}) copy-start(f32[128,128]{0,1:T(8,128)S(1)} %get-tuple-element.474) | copy-start | bytes 196612
  9.3 205.0 %copy-start.40 = (f32[128,128]{0,1:T(8,128)}, f32[128,128]{0,1:T(8,128)S(1)}, u32[]{:S(2)}) copy-start(f32[128,128]{0,1:T(8,128)S(1)} %get-tuple-element.475) | copy-start | bytes 196612
  9.4 257.6 %copy-start.34 = (f32[128,128]{1,0:T(8,128)}, f32[128,128]{1,0:T(8,128)S(1)}, u32[]{:S(2)}) copy-start(f32[128,128]{1,0:T(8,128)S(1)} %copy.294) | copy-start | bytes 196612
  9.5 257.5 %copy-start.38 = (f32[128,128]{1,0:T(8,128)}, f32[128,128]{1,0:T(8,128)S(1)}, u32[]{:S(2)}) copy-start(f32[128,128]{1,0:T(8,128)S(1)} %copy.295) | copy-start | bytes 196612
  21.4 192.8 %copy-start.75 = (f32[128]{0:T(128)}, f32[128]{0:T(128)S(1)}, u32[]{:S(2)}) copy-start(f32[128]{0:T(128)S(1)} %get-tuple-element.465) | copy-start | bytes 1540
  221.7 45.3 %copy-start.54 = (f32[128,32]{0,1:T(8,128)}, f32[128,32]{0,1:T(8,128)S(1)}, u32[]{:S(2)}) copy-start(f32[128,32]{0,1:T(8,128)S(1)} %copy.298) | copy-start | bytes 49156
  232.3 34.7 %copy-start.83 = (f32[128]{0:T(128)S(1)}, f32[128]{0:T(128)}, u32[]{:S(2)}) copy-start(f32[128]{0:T(128)} %param.21) | copy-start | bytes 1540
  233.4 37.0 %copy-start.27 = (f32[16,4,8,128]{3,2,1,0:T(8,128)}, f32[16,4,8,128]{3,2,1,0:T(8,128)S(1)}, u32[]{:S(2)}) copy-start(f32[16,4,8,128]{3,2,1,0:T(8,128)S(1)} %get-tuple-element.445) | copy-start | bytes 786436
  233.8 33.3 %copy-start.26 = (f32[16,8,32,128]{3,2,1,0:T(8,128)S(1)}, f32[16,8,32,128]{3,2,1,0:T(8,128)}, u32[]{:S(2)}) copy-start(f32[16,8,32,128]{3,2,1,0:T(8,128)} %copy.347) | copy-start | bytes 6291460
  234.4 36.0 %copy-start.71 = (f32[128,4]{0,1:T(4,128)}, f32[128,4]{0,1:T(4,128)S(1)}, u32[]{:S(2)}) copy-start(f32[128,4]{0,1:T(4,128)S(1)} %get-tuple-element.461) | copy-start | bytes 6148
  270.4 102.9 %copy-start.16 = (bf16[128,2048]{1,0:T(8,128)(2,1)S(1)}, bf16[128,2048]{1,0:T(8,128)(2,1)}, u32[]{:S(2)}) copy-start(bf16[128,2048]{1,0:T(8,128)(2,1)} %param.16) | copy-start | bytes 1572868
  286.1 95.4 %copy-start.3 = (bf16[4,128,8,128]{1,3,2,0:T(8,128)(2,1)}, bf16[4,128,8,128]{1,3,2,0:T(8,128)(2,1)S(1)}, u32[]{:S(2)}) copy-start(bf16[4,128,8,128]{1,3,2,0:T(8,128)(2,1)S(1)} %get-tuple-element.706) | copy-start | bytes 3145732
  286.1 95.4 %copy-start.18 = (bf16[4,128,8,128]{3,1,2,0:T(8,128)(2,1)}, bf16[4,128,8,128]{3,1,2,0:T(8,128)(2,1)S(1)}, u32[]{:S(2)}) copy-start(bf16[4,128,8,128]{3,1,2,0:T(8,128)(2,1)S(1)} %get-tuple-element.766) | copy-start | bytes 3145732
  286.1 95.4 %copy-start.67 = (s32[128]{0:T(128)}, s32[128]{0:T(128)S(1)}, u32[]{:S(2)}) copy-start(s32[128]{0:T(128)S(1)} %get-tuple-element.791) | copy-start | bytes 1540
  286.1 95.4 %copy-start.69 = (s32[128]{0:T(128)}, s32[128]{0:T(128)S(1)}, u32[]{:S(2)}) copy-start(s32[128]{0:T(128)S(1)} %get-tuple-element.792) | copy-start | bytes 1540
  397.7 391.6 %slice-start.2 = ((s8[9437184]{0:T(1024)(128)(4,1)}), s8[1048576]{0:T(1024)(128)(4,1)S(1)}, s32[]{:S(2)}) async-start(s8[9437184]{0:T(1024)(128)(4,1)} %bitcast.414), calls=%async_computation.16 | async-start | bytes 2097152
  420.5 368.8 %slice-start.3 = ((s8[9437184]{0:T(1024)(128)(4,1)}), s8[4194304]{0:T(1024)(128)(4,1)S(1)}, s32[]{:S(2)}) async-start(s8[9437184]{0:T(1024)(128)(4,1)} %bitcast.414), calls=%async_computation.17 | async-start | bytes 8388608
  420.5 368.8 %slice-start.4 = ((s8[9437184]{0:T(1024)(128)(4,1)}), s8[4194304]{0:T(1024)(128)(4,1)S(1)}, s32[]{:S(2)}) async-start(s8[9437184]{0:T(1024)(128)(4,1)} %bitcast.414), calls=%async_computation.18 | async-start | bytes 8388608
  825.6 11.6 copy-start.94
  1073.7 386.5 %all-to-all-start.1 = ((bf16[32,2,131072]{2,1,0:T(2,128)(2,1)}), bf16[32,2,131072]{2,1,0:T(2,128)(2,1)}, u32[]{:S(2)}, u32[]{:S(2)}) async-start(bf16[32,2,131072]{2,1,0:T(2,128)(2,1)} %reshape.465), calls=%async_computation.1 | async-start | bytes 33554432 | tf_op jit(solution)/shard_map/all_to_all | solution.py:276
  1077.7 584.7 %reduce-scatter.5.cloned.1.call-start = ((), (), s32[]{:S(2)}) async-start(), calls=%async_computation.8 | async-start | bytes 655360 | tf_op jit(solution)/shard_map/reduce_scatter | solution.py:306
  1522.2 23.1 copy-start.22
  1522.2 23.1 copy-start.43
  1545.3 11.1 copy-start.66
  1545.3 11.1 copy-start.60
  1545.3 11.1 copy-start.79
  1545.3 11.1 copy-start.86
  1545.3 11.2 copy-start.14
  1545.3 11.2 copy-start.57
  1545.4 11.2 copy-start.64
  1545.4 11.2 copy-start.90
  1560.9 11.8 copy-start.10
  1622.1 48.9 %reduce-scatter.7.cloned.1.call-start = ((), (), s32[]{:S(2)}) async-start(), calls=%async_computation.9 | async-start | bytes 655360 | tf_op jit(solution)/shard_map/reduce_scatter | solution.py:309
  1622.7 205.0 %reduce-scatter.11.cloned.1.call-start = ((), (), s32[]{:S(2)}) async-start(), calls=%async_computation.11 | async-start | bytes 20971520 | tf_op jit(solution)/shard_map/reduce_scatter | solution.py:291
  1634.6 383.8 %reduce-scatter.9.cloned.1.call-start = ((), (), s32[]{:S(2)}) async-start(), calls=%async_computation.10 | async-start | bytes 26214400 | tf_op jit(solution)/shard_map/reduce_scatter | solution.py:321
  1642.0 11.7 copy-start.7
  1654.3 17.7 copy-start.80
  1682.7 534.5 %all-reduce.7.cloned.1.call-start = ((), (), s32[]{:S(2)}) async-start(), calls=%async_computation.13 | async-start | bytes 18874368 | tf_op jit(solution)/shard_map/psum | solution.py:336
  2018.5 331.6 %all-reduce.5.cloned.1.call-start = ((), (), s32[]{:S(2)}) async-start(), calls=%async_computation.12 | async-start | bytes 524288 | tf_op jit(solution)/shard_map/psum | solution.py:332
  2018.5 20.4 slice-start
  2058.8 12.1 copy-start.11
  2058.8 12.1 copy-start.91
  (74 other events, 328.8 us)
Sparse Core Ops, SparseCore 0:
  9.9 195.7 all-gather.2
  207.5 165.7 all-gather.4
  1622.2 20.9 reduce-scatter.4
  1645.9 25.0 reduce-scatter.6
  1673.9 153.7 reduce-scatter.10
  1830.7 187.7 reduce-scatter.8
  2020.9 196.3 all-reduce.6
  2223.3 126.6 all-reduce.4
where the time goes:
time: 2370 us; the launch traced here: 2360 us
  waiting for transfers between devices  1210 us (51%)
  blocking collectives  441 us (19%)
  local copies, waits for them, and re-layouts  274 us (12%)
  matrix products  209 us (9%)
  other arithmetic  207 us (9%)
    all_to_all x1, waiting for transfers between devices, body(): lax.all_to_all(outgoing, ('rep', 'shard'), split_axis=1, concat_axis=0, t...  382 us
    all_to_all x1, blocking collectives, body(): lax.all_to_all(buffer, ('rep', 'shard'), split_axis=0, concat_axis=1, til...  369 us
    reduce_scatter x1, waiting for transfers between devices, body(): lax.psum_scatter(lax.dot_general(columns, grad_qkv_b, (((0,), (0,)), ((),...  191 us
    all_gather x1, waiting for transfers between devices, body(): lax.all_gather(query_key_value_weight, 'shard', axis=0, tiled=True)  184 us
    dot_general x37, matrix products, product(): return jnp.einsum(form, left, right, preferred_element_type=jnp.float32)  143 us
    reduce_scatter x1, waiting for transfers between devices, body(): lax.psum_scatter(lax.dot_general(columns, grad_middle_b, (((0,), (0,)), (...  130 us
    psum x1, waiting for transfers between devices, body(): lax.psum((grad_attn_gain, grad_q_gain, grad_k_gain, grad_ffn_gain, grad_r...  120 us
    unnamed x205, local copies, waits for them, and re-layouts  105 us
  transfers between devices with their start and end apart: 9, of which 8 were waited for; matrix products, arithmetic and copies ran while one was open for 8% of the time, Pallas kernels for 0%

commit v1 on v0

--- a/solution.py
+++ b/solution.py
@@ -1,7 +1,12 @@
+import functools
+
 import jax
 import jax.numpy as jnp
 from jax import lax
+from jax.experimental import pallas as pl
+from jax.experimental.pallas import tpu as pltpu
 from jax.sharding import PartitionSpec as P
+
 
 QUERY_HEADS = 32
 KEY_VALUE_HEADS = 4
@@ -211,7 +216,7 @@
     )
 
 
-def body(
+def plain_body(
     block_in,
     segments,
     routes,
@@ -350,6 +355,909 @@
     )
 
 
+MESH_ID = pl.DeviceIdType.MESH
+PLANES = 4
+
+
+def place():
+    rep, shard = lax.axis_index("rep"), lax.axis_index("shard")
+    return rep // 2, rep % 2, shard // 2, shard % 2
+
+
+def device(z, core, y, x):
+    return (z * 2 + core, y * 2 + x)
+
+
+def block_of(z, core, y, x):
+    return (z * 2 + core) * 4 + y * 2 + x
+
+
+def greet(targets):
+    barrier = pltpu.get_barrier_semaphore()
+    for condition, target in targets:
+        if condition is None:
+            pl.semaphore_signal(barrier, inc=1, device_id=target, device_id_type=MESH_ID)
+        else:
+
+            @pl.when(condition)
+            def _():
+                pl.semaphore_signal(barrier, inc=1, device_id=target, device_id_type=MESH_ID)
+
+    peers = 0
+    for condition, _ in targets:
+        peers = peers + (1 if condition is None else condition.astype(jnp.int32))
+    pl.semaphore_wait(barrier, peers)
+
+
+def gather_kernel(rows, *refs):
+    count = len(rows)
+    ins, outs = refs[:count], refs[count : 2 * count]
+    send_sem, recv_sem, own_sem = refs[2 * count :]
+    z, core, y, x = place()
+    partner = device(z, 1 - core, y, x)
+    x_next, y_next = device(z, core, y, 1 - x), device(z, core, 1 - y, x)
+    up, down = device(z + 1, core, y, x), device(z - 1, core, y, x)
+    greet(
+        [
+            (None, partner),
+            (None, x_next),
+            (None, y_next),
+            (z < PLANES - 1, up),
+            (z > 0, down),
+        ]
+    )
+    pending, used = [], [0]
+    can_up, can_down = z < PLANES - 1, z > 0
+
+    def region(array, block, part):
+        size = rows[array]
+        if part is None:
+            return pl.ds(pl.multiple_of(block * size, size), size)
+        return pl.ds(pl.multiple_of(block * size + part * (size // 2), size // 2), size // 2)
+
+    def copy_of(array, block, part, target, index, own=False):
+        where = region(array, block, part)
+        source = ins[array] if own else outs[array].at[where]
+        return pltpu.make_async_remote_copy(
+            src_ref=source,
+            dst_ref=outs[array].at[where],
+            send_sem=send_sem.at[array, index],
+            recv_sem=recv_sem.at[array, block * 2 + (part or 0)],
+            device_id=target,
+            device_id_type=MESH_ID,
+        )
+
+    def send(block, part, target, condition=None, own=False, guard=None):
+        index = used[0]
+        used[0] += 1
+
+        def start():
+            for array in range(count):
+                copy_of(array, block, part, target, index, own).start()
+
+        def finish():
+            for array in range(count):
+                copy_of(array, block, part, target, index, own).wait_send()
+
+        if condition is None:
+            start()
+        else:
+            pl.when(condition)(start)
+        pending.append(([c for c in (guard, condition) if c is not None], finish))
+
+    def arrived(block, part):
+        for array in range(count):
+            copy_of(array, block, part, partner, 0).wait_recv()
+
+    own = block_of(z, core, y, x)
+    send(own, None, up, can_up, own=True)
+    send(own, None, down, can_down, own=True)
+    send(own, None, x_next, own=True)
+    send(own, None, y_next, own=True)
+    send(own, None, partner, own=True)
+    for array in range(count):
+        pltpu.make_async_copy(
+            ins[array], outs[array].at[region(array, own, None)], own_sem.at[array]
+        ).start()
+
+    def planes(step):
+        if step == 0:
+            return [(None, z)]
+        return [(z >= step, z - step), (z + step < PLANES, z + step)]
+
+    def under(condition, run):
+        if condition is None:
+            run()
+        else:
+            pl.when(condition)(run)
+
+    def along_z(step):
+        for side, (condition, plane) in enumerate(planes(step)):
+            block = block_of(plane, core, y, x)
+
+            def run():
+                arrived(block, None)
+                if side == 0:
+                    send(block, None, up, can_up, guard=condition)
+                else:
+                    send(block, None, down, can_down, guard=condition)
+                send(block, None, x_next, guard=condition)
+                send(block, None, y_next, guard=condition)
+                send(block, None, partner, guard=condition)
+
+            under(condition, run)
+
+    def across(step):
+        for condition, plane in planes(step):
+            from_x, from_y = block_of(plane, core, y, 1 - x), block_of(plane, core, 1 - y, x)
+
+            def run():
+                arrived(from_x, None)
+                send(from_x, 1, y_next, guard=condition)
+                send(from_x, None, partner, guard=condition)
+                arrived(from_y, None)
+                send(from_y, 0, x_next, guard=condition)
+                send(from_y, None, partner, guard=condition)
+
+            under(condition, run)
+
+    def diagonal(step):
+        for condition, plane in planes(step):
+            block = block_of(plane, core, 1 - y, 1 - x)
+
+            def run():
+                for part in range(2):
+                    arrived(block, part)
+                    send(block, part, partner, guard=condition)
+
+            under(condition, run)
+
+    along_z(1)
+    across(0)
+    along_z(2)
+    across(1)
+    along_z(3)
+    diagonal(0)
+    across(2)
+    diagonal(1)
+    across(3)
+    diagonal(2)
+    diagonal(3)
+    for plane in range(PLANES):
+        for where_y, where_x in ((y, x), (y, 1 - x), (1 - y, x)):
+            arrived(block_of(plane, 1 - core, where_y, where_x), None)
+        for part in range(2):
+            arrived(block_of(plane, 1 - core, 1 - y, 1 - x), part)
+    for array in range(count):
+        pltpu.make_async_copy(
+            ins[array], outs[array].at[region(array, own, None)], own_sem.at[array]
+        ).wait()
+    for conditions, finish in pending:
+        if len(conditions) == 2:
+            under(jnp.logical_and(*conditions), finish)
+        else:
+            under(conditions[0] if conditions else None, finish)
+
+
+def gather_all(arrays, collective_id):
+    rows = tuple(array.shape[0] for array in arrays)
+    count = len(arrays)
+    return pl.pallas_call(
+        functools.partial(gather_kernel, rows),
+        out_shape=[
+            jax.ShapeDtypeStruct((array.shape[0] * 32,) + array.shape[1:], array.dtype)
+            for array in arrays
+        ],
+        in_specs=[pl.BlockSpec(memory_space=pltpu.VMEM)] * count,
+        out_specs=[pl.BlockSpec(memory_space=pltpu.HBM)] * count,
+        scratch_shapes=[
+            pltpu.SemaphoreType.DMA((count, 72)),
+            pltpu.SemaphoreType.DMA((count, 64)),
+            pltpu.SemaphoreType.DMA((count,)),
+        ],
+        compiler_params=pltpu.CompilerParams(
+            collective_id=collective_id, has_side_effects=True, vmem_limit_bytes=40 << 20
+        ),
+        name="gather_all",
+    )(*arrays)
+
+
+def add_rows(target, sources, rows=128, step=16):
+    @pl.loop(0, rows // step)
+    def _(i):
+        where = pl.ds(pl.multiple_of(i * step, step), step)
+        total = target[where].astype(jnp.float32)
+        for source in sources:
+            total += source[where].astype(jnp.float32)
+        target[where] = total.astype(target.dtype)
+
+
+def reduce_kernel(
+    part_ref,
+    out_ref,
+    kept,
+    paired,
+    x_half,
+    x_full,
+    y_half,
+    y_full,
+    from_up,
+    from_down,
+    send_sem,
+    pair_sem,
+    x_sem,
+    y_sem,
+    z_sem,
+    load_sem,
+):
+    rows = out_ref.shape[0]
+    half = rows // 2
+    z, core, y, x = place()
+    partner = device(z, 1 - core, y, x)
+    x_next, y_next = device(z, core, y, 1 - x), device(z, core, 1 - y, x)
+    up, down = device(z + 1, core, y, x), device(z - 1, core, y, x)
+    greet(
+        [
+            (None, partner),
+            (None, x_next),
+            (None, y_next),
+            (z < PLANES - 1, up),
+            (z > 0, down),
+        ]
+    )
+    pending, used = [], [0]
+
+    def send(source, landing, sem, target, condition=None):
+        copy = pltpu.make_async_remote_copy(
+            src_ref=source,
+            dst_ref=landing,
+            send_sem=send_sem.at[used[0]],
+            recv_sem=sem,
+            device_id=target,
+            device_id_type=MESH_ID,
+        )
+        used[0] += 1
+        if condition is None:
+            copy.start()
+        pending.append((condition, copy))
+        return copy
+
+    def arrived(landing, sem):
+        pltpu.make_async_remote_copy(
+            src_ref=landing,
+            dst_ref=landing,
+            send_sem=send_sem.at[0],
+            recv_sem=sem,
+            device_id=partner,
+            device_id_type=MESH_ID,
+        ).wait_recv()
+
+    order = (0, 3, 1, 2)
+    spots = ((1 - y, 1 - x), (y, 1 - x), (1 - y, x), (y, x))
+
+    def slot(plane, spot):
+        return plane * 4 + spots[spot][0] * 2 + spots[spot][1]
+
+    def block(plane, which, spot):
+        size = pl.multiple_of(block_of(plane, which, *spots[spot]) * rows, rows)
+        return part_ref.at[pl.ds(size, rows)]
+
+    def load(plane, spot):
+        return pltpu.make_async_copy(
+            block(plane, core, spot), kept.at[slot(plane, spot)], load_sem.at[spot * 4 + plane]
+        )
+
+    for spot in range(4):
+        for plane in order:
+            where = slot(plane, spot)
+            send(block(plane, 1 - core, spot), paired.at[where], pair_sem.at[where], partner)
+            load(plane, spot).start()
+
+    def joined(plane, spot, more=()):
+        where = slot(plane, spot)
+        load(plane, spot).wait()
+        arrived(paired.at[where], pair_sem.at[where])
+        add_rows(kept.at[where], (paired.at[where],) + tuple(more), rows)
+
+    for plane in order:
+        joined(plane, 0)
+        source = kept.at[slot(plane, 0)]
+        send(source.at[pl.ds(0, half)], x_half.at[plane], x_sem.at[plane], x_next)
+        send(source.at[pl.ds(half, half)], y_half.at[plane], y_sem.at[plane], y_next)
+    for plane in order:
+        joined(plane, 1)
+        arrived(y_half.at[plane], y_sem.at[plane])
+        add_rows(kept.at[slot(plane, 1)].at[pl.ds(half, half)], (y_half.at[plane],), half)
+        send(kept.at[slot(plane, 1)], x_full.at[plane], x_sem.at[4 + plane], x_next)
+        joined(plane, 2)
+        arrived(x_half.at[plane], x_sem.at[plane])
+        add_rows(kept.at[slot(plane, 2)].at[pl.ds(0, half)], (x_half.at[plane],), half)
+        send(kept.at[slot(plane, 2)], y_full.at[plane], y_sem.at[4 + plane], y_next)
+    for plane in order:
+        arrived(x_full.at[plane], x_sem.at[4 + plane])
+        arrived(y_full.at[plane], y_sem.at[4 + plane])
+        joined(plane, 3, (x_full.at[plane], y_full.at[plane]))
+        total = kept.at[slot(plane, 3)]
+        if plane < PLANES - 1:
+            copy = send(total, from_up.at[plane], z_sem.at[0, plane], down, z > plane)
+
+            @pl.when(z > plane)
+            def _():
+                @pl.when(z < PLANES - 1)
+                def _():
+                    arrived(from_up.at[plane], z_sem.at[0, plane])
+                    add_rows(total, (from_up.at[plane],), rows)
+
+                copy.start()
+
+        if plane > 0:
+            climb = send(total, from_down.at[plane - 1], z_sem.at[1, plane - 1], up, z < plane)
+
+            @pl.when(z < plane)
+            def _():
+                @pl.when(z > 0)
+                def _():
+                    arrived(from_down.at[plane - 1], z_sem.at[1, plane - 1])
+                    add_rows(total, (from_down.at[plane - 1],), rows)
+
+                climb.start()
+
+    mine = kept.at[slot(z, 3)]
+
+    @pl.when(z < PLANES - 1)
+    def _():
+        arrived(from_up.at[z], z_sem.at[0, z])
+        add_rows(mine, (from_up.at[z],), rows)
+
+    @pl.when(z > 0)
+    def _():
+        arrived(from_down.at[z - 1], z_sem.at[1, z - 1])
+        add_rows(mine, (from_down.at[z - 1],), rows)
+
+    out_ref[...] = mine[...]
+    for condition, copy in pending:
+        if condition is None:
+            copy.wait_send()
+        else:
+            pl.when(condition)(copy.wait_send)
+
+
+def reduce_all(part, collective_id):
+    total, width = part.shape
+    rows = total // 32
+    half = rows // 2
+    dtype = part.dtype
+    return pl.pallas_call(
+        reduce_kernel,
+        out_shape=jax.ShapeDtypeStruct((rows, width), dtype),
+        in_specs=[pl.BlockSpec(memory_space=pltpu.HBM)],
+        out_specs=pl.BlockSpec(memory_space=pltpu.VMEM),
+        scratch_shapes=[
+            pltpu.VMEM((16, rows, width), dtype),
+            pltpu.VMEM((16, rows, width), dtype),
+            pltpu.VMEM((4, half, width), dtype),
+            pltpu.VMEM((4, rows, width), dtype),
+            pltpu.VMEM((4, half, width), dtype),
+            pltpu.VMEM((4, rows, width), dtype),
+            pltpu.VMEM((3, rows, width), dtype),
+            pltpu.VMEM((3, rows, width), dtype),
+            pltpu.SemaphoreType.DMA((48,)),
+            pltpu.SemaphoreType.DMA((16,)),
+            pltpu.SemaphoreType.DMA((8,)),
+            pltpu.SemaphoreType.DMA((8,)),
+            pltpu.SemaphoreType.DMA((2, 3)),
+            pltpu.SemaphoreType.DMA((16,)),
+        ],
+        compiler_params=pltpu.CompilerParams(
+            collective_id=collective_id, has_side_effects=True, vmem_limit_bytes=60 << 20
+        ),
+        name="reduce_all",
+    )(part)
+
+
+def others():
+    z, core, y, x = place()
+    return [
+        (device(z, core, yy, xx), yy * 2 + xx)
+        for yy, xx in ((y, 1 - x), (1 - y, x), (1 - y, 1 - x))
+    ]
+
+
+def remote(source, landing, send_sem, recv_sem, target):
+    return pltpu.make_async_remote_copy(
+        src_ref=source,
+        dst_ref=landing,
+        send_sem=send_sem,
+        recv_sem=recv_sem,
+        device_id=target,
+        device_id_type=MESH_ID,
+    )
+
+
+def start_kernel(
+    x_ref, w_ref, x_all, w_own, hold, send_sem, x_sem, w_sem, pair_sem, own_sem
+):
+    tok = x_ref.shape[0]
+    depth = w_ref.shape[0]
+    half = depth // 2
+    z, core, y, x = place()
+    me = y * 2 + x
+    partner = device(z, 1 - core, y, x)
+    near = others()
+    greet([(None, target) for target, _ in near] + [(None, partner)])
+    parts = QUERY_HEADS // 4 * HEAD_SIZE
+    single = HEAD_SIZE
+    widths = (
+        (0, parts, 0),
+        (QUERY_HEADS * HEAD_SIZE, single, parts),
+        ((QUERY_HEADS + KEY_VALUE_HEADS) * HEAD_SIZE, single, parts + single),
+    )
+
+    def columns(piece, who):
+        base, width, _ = widths[piece]
+        return pl.ds(pl.multiple_of(base + who * width, 128), width)
+
+    def landing(piece, who, part, ref=w_own):
+        _, width, offset = widths[piece]
+        rows = pl.ds(pl.multiple_of(who * depth + part * half, half), half)
+        return ref.at[rows, pl.ds(offset, width)]
+
+    sends = []
+    for slot, (target, who) in enumerate(near):
+        for piece in range(3):
+            copy = remote(
+                w_ref.at[pl.ds(pl.multiple_of(core * half, half), half), columns(piece, who)],
+                landing(piece, me, core),
+                send_sem.at[slot * 4 + piece],
+                w_sem.at[slot * 3 + piece],
+                target,
+            )
+            copy.start()
+            sends.append(copy)
+        copy = remote(
+            x_ref,
+            x_all.at[pl.ds(pl.multiple_of(me * tok, tok), tok)],
+            send_sem.at[slot * 4 + 3],
+            x_sem.at[slot],
+            target,
+        )
+        copy.start()
+        sends.append(copy)
+    mine = pltpu.make_async_copy(
+        x_ref, x_all.at[pl.ds(pl.multiple_of(me * tok, tok), tok)], own_sem.at[0]
+    )
+    mine.start()
+    loads = []
+    for piece in range(3):
+        _, width, offset = widths[piece]
+        loads.append(
+            pltpu.make_async_copy(
+                w_ref.at[:, columns(piece, me)], hold.at[:, pl.ds(offset, width)], own_sem.at[1 + piece]
+            )
+        )
+        loads[-1].start()
+    for copy in loads:
+        copy.wait()
+    keep = pltpu.make_async_copy(
+        hold, w_own.at[pl.ds(pl.multiple_of(me * depth, depth), depth)], own_sem.at[4]
+    )
+    keep.start()
+    for slot, (target, who) in enumerate(near):
+        for piece in range(3):
+            where = landing(piece, who, core)
+            remote(where, where, send_sem.at[0], w_sem.at[slot * 3 + piece], partner).wait_recv()
+        rows = w_own.at[pl.ds(pl.multiple_of(who * depth + core * half, half), half)]
+        copy = remote(rows, rows, send_sem.at[12 + slot], pair_sem.at[slot], partner)
+        copy.start()
+        sends.append(copy)
+    for slot, (target, who) in enumerate(near):
+        rows = w_own.at[pl.ds(pl.multiple_of(who * depth + (1 - core) * half, half), half)]
+        remote(rows, rows, send_sem.at[0], pair_sem.at[slot], partner).wait_recv()
+        rows = x_all.at[pl.ds(pl.multiple_of(who * tok, tok), tok)]
+        remote(rows, rows, send_sem.at[0], x_sem.at[slot], partner).wait_recv()
+    mine.wait()
+    keep.wait()
+    for copy in sends:
+        copy.wait_send()
+
+
+def start_exchange(block_in, weight, collective_id):
+    tok, width = block_in.shape
+    depth, columns = weight.shape
+    return pl.pallas_call(
+        start_kernel,
+        out_shape=[
+            jax.ShapeDtypeStruct((tok * 4, width), block_in.dtype),
+            jax.ShapeDtypeStruct((depth * 4, columns // 4), weight.dtype),
+        ],
+        in_specs=[
+            pl.BlockSpec(memory_space=pltpu.VMEM),
+            pl.BlockSpec(memory_space=pltpu.HBM),
+        ],
+        out_specs=[pl.BlockSpec(memory_space=pltpu.HBM)] * 2,
+        scratch_shapes=[
+            pltpu.VMEM((depth, columns // 4), weight.dtype),
+            pltpu.SemaphoreType.DMA((16,)),
+            pltpu.SemaphoreType.DMA((3,)),
+            pltpu.SemaphoreType.DMA((9,)),
+            pltpu.SemaphoreType.DMA((3,)),
+            pltpu.SemaphoreType.DMA((5,)),
+        ],
+        compiler_params=pltpu.CompilerParams(
+            collective_id=collective_id, has_side_effects=True, vmem_limit_bytes=40 << 20
+        ),
+        name="start_exchange",
+    )(block_in, weight)
+
+
+def spread_kernel(x_ref, x_all, send_sem, x_sem, own_sem):
+    tok = x_ref.shape[0]
+    z, core, y, x = place()
+    me = y * 2 + x
+    near = others()
+    greet([(None, target) for target, _ in near])
+    sends = []
+    rows = x_all.at[pl.ds(pl.multiple_of(me * tok, tok), tok)]
+    for slot, (target, _) in enumerate(near):
+        copy = remote(x_ref, rows, send_sem.at[slot], x_sem.at[slot], target)
+        copy.start()
+        sends.append(copy)
+    mine = pltpu.make_async_copy(x_ref, rows, own_sem)
+    mine.start()
+    for slot, (target, who) in enumerate(near):
+        rows = x_all.at[pl.ds(pl.multiple_of(who * tok, tok), tok)]
+        remote(rows, rows, send_sem.at[0], x_sem.at[slot], target).wait_recv()
+    mine.wait()
+    for copy in sends:
+        copy.wait_send()
+
+
+def spread_sequence(rows, collective_id):
+    tok, width = rows.shape
+    return pl.pallas_call(
+        spread_kernel,
+        out_shape=jax.ShapeDtypeStruct((tok * 4, width), rows.dtype),
+        in_specs=[pl.BlockSpec(memory_space=pltpu.VMEM)],
+        out_specs=pl.BlockSpec(memory_space=pltpu.HBM),
+        scratch_shapes=[
+            pltpu.SemaphoreType.DMA((3,)),
+            pltpu.SemaphoreType.DMA((3,)),
+            pltpu.SemaphoreType.DMA,
+        ],
+        compiler_params=pltpu.CompilerParams(
+            collective_id=collective_id, has_side_effects=True, vmem_limit_bytes=40 << 20
+        ),
+        name="spread_sequence",
+    )(rows)
+
+
+def fold_kernel(part_ref, out_ref, landing, send_sem, recv_sem):
+    tok = out_ref.shape[0]
+    z, core, y, x = place()
+    me = y * 2 + x
+    near = others()
+    greet([(None, target) for target, _ in near])
+    sends = []
+    for slot, (target, who) in enumerate(near):
+        copy = remote(
+            part_ref.at[pl.ds(pl.multiple_of(who * tok, tok), tok)],
+            landing.at[slot],
+            send_sem.at[slot],
+            recv_sem.at[slot],
+            target,
+        )
+        copy.start()
+        sends.append(copy)
+    for slot, (target, _) in enumerate(near):
+        remote(
+            landing.at[slot], landing.at[slot], send_sem.at[0], recv_sem.at[slot], target
+        ).wait_recv()
+
+    @pl.loop(0, tok // 16)
+    def _(i):
+        where = pl.ds(pl.multiple_of(i * 16, 16), 16)
+        total = part_ref[pl.ds(pl.multiple_of(me * tok + i * 16, 16), 16)].astype(jnp.float32)
+        for slot in range(3):
+            total += landing[slot, where].astype(jnp.float32)
+        out_ref[where] = total
+
+    for copy in sends:
+        copy.wait_send()
+
+
+def fold_sequence(part, collective_id):
+    total, width = part.shape
+    tok = total // 4
+    return pl.pallas_call(
+        fold_kernel,
+        out_shape=jax.ShapeDtypeStruct((tok, width), jnp.float32),
+        in_specs=[pl.BlockSpec(memory_space=pltpu.VMEM)],
+        out_specs=pl.BlockSpec(memory_space=pltpu.VMEM),
+        scratch_shapes=[
+            pltpu.VMEM((3, tok, width), part.dtype),
+            pltpu.SemaphoreType.DMA((3,)),
+            pltpu.SemaphoreType.DMA((3,)),
+        ],
+        compiler_params=pltpu.CompilerParams(
+            collective_id=collective_id, has_side_effects=True, vmem_limit_bytes=40 << 20
+        ),
+        name="fold_sequence",
+    )(part)
+
+
+def expert_kernel(
+    slots_ref,
+    gates_ref,
+    x_ref,
+    g_ref,
+    w_ref,
+    out_ref,
+    grad_ref,
+    gg_ref,
+    grad_w,
+    xs,
+    gs,
+    weighted,
+    sums,
+    sem,
+):
+    step = pl.program_id(0)
+    blocks = x_ref.shape[0] // 128
+    cap = xs.shape[0] // blocks
+
+    @pl.when(step == 0)
+    def _():
+        sums[...] = jnp.zeros_like(sums)
+
+    def dot(left, right, dims):
+        return lax.dot_general(
+            left, right, ((dims[:1], dims[1:]), ((), ())), preferred_element_type=jnp.float32
+        )
+
+    chosen, gate_rows = [], []
+    for pair in range(blocks // 2):
+        slot_row = jnp.concatenate(
+            [
+                slots_ref[pl.ds(step * blocks + pair * 2, 1), :],
+                slots_ref[pl.ds(step * blocks + pair * 2 + 1, 1), :] + float(cap),
+            ],
+            axis=1,
+        )
+        gate_row = jnp.concatenate(
+            [gates_ref[pl.ds(step * blocks + pair * 2 + j, 1), :] for j in range(2)], axis=1
+        )
+        ids = lax.broadcasted_iota(jnp.int32, (2 * cap, 256), 0).astype(jnp.float32)
+        mask = jnp.where(ids == slot_row, 1.0, 0.0)
+        pick = mask.astype(jnp.bfloat16)
+        rows = pl.ds(pair * 2 * cap, 2 * cap)
+        tokens = pl.ds(pair * 256, 256)
+        gate = jnp.sum(mask * gate_row, axis=1, keepdims=True)
+        xs[rows] = dot(pick, x_ref[tokens], (1, 0)).astype(jnp.bfloat16)
+        upstream = dot(pick, g_ref[tokens], (1, 0))
+        gs[rows] = upstream.astype(jnp.bfloat16)
+        weighted[rows] = (upstream * gate).astype(jnp.bfloat16)
+        chosen.append(pick)
+        gate_rows.append(gate)
+    rows_x = xs[...]
+    rows_g = weighted[...]
+    gate_pre = dot(rows_x, w_ref[0], (1, 0))
+    up_pre = dot(rows_x, w_ref[1], (1, 0))
+    sig = jax.nn.sigmoid(gate_pre)
+    silu = gate_pre * sig
+    hidden = (silu * up_pre).astype(jnp.bfloat16)
+    grad_hidden = dot(rows_g, w_ref[2], (1, 0))
+    grad_gate = (grad_hidden * up_pre * sig * (1.0 + gate_pre * (1.0 - sig))).astype(jnp.bfloat16)
+    grad_up = (grad_hidden * silu).astype(jnp.bfloat16)
+    result = dot(hidden, w_ref[2], (1, 1)).astype(jnp.bfloat16)
+    grad_in = (dot(grad_gate, w_ref[0], (1, 1)) + dot(grad_up, w_ref[1], (1, 1))).astype(
+        jnp.bfloat16
+    )
+    sums[0] += dot(rows_x, grad_gate, (0, 0))
+    sums[1] += dot(rows_x, grad_up, (0, 0))
+    sums[2] += dot(rows_g, hidden, (0, 0))
+    result_f = result.astype(jnp.float32)
+    along = jnp.sum(gs[...].astype(jnp.float32) * result_f, axis=1, keepdims=True)
+    for pair in range(blocks // 2):
+        tokens = pl.ds(pair * 256, 256)
+        low, high = pair * 2 * cap, (pair + 1) * 2 * cap
+        pick = chosen[pair]
+        scaled = (result_f[low:high] * gate_rows[pair]).astype(jnp.bfloat16)
+        out_ref[tokens] = dot(pick, scaled, (0, 0)).astype(jnp.bfloat16)
+        grad_ref[tokens] = dot(pick, grad_in[low:high], (0, 0)).astype(jnp.bfloat16)
+        row = jnp.sum(pick.astype(jnp.float32) * along[low:high], axis=0, keepdims=True)
+        for j in range(2):
+            gg_ref[pl.ds(step * blocks + pair * 2 + j, 1), :] = row[:, j * 128 : (j + 1) * 128]
+
+    @pl.when(step == pl.num_programs(0) - 1)
+    def _():
+        copy = pltpu.make_async_copy(sums, grad_w.at[0], sem)
+        copy.start()
+        copy.wait()
+
+
+def run_expert(slots, gates, tokens, upstream, weights, cap):
+    count, width = tokens.shape
+    _, three, _, ff = weights.shape
+    group = 512
+    steps = count // group
+    held = group // 128 * cap
+    whole = lambda i: (0, 0)
+    return pl.pallas_call(
+        expert_kernel,
+        grid=(steps,),
+        out_shape=[
+            jax.ShapeDtypeStruct((count, width), jnp.bfloat16),
+            jax.ShapeDtypeStruct((count, width), jnp.bfloat16),
+            jax.ShapeDtypeStruct(slots.shape, jnp.float32),
+            jax.ShapeDtypeStruct(weights.shape, jnp.float32),
+        ],
+        in_specs=[
+            pl.BlockSpec(slots.shape, whole),
+            pl.BlockSpec(gates.shape, whole),
+            pl.BlockSpec((group, width), lambda i: (i, 0)),
+            pl.BlockSpec((group, width), lambda i: (i, 0)),
+            pl.BlockSpec(
+                (None, three, width, ff), lambda i: (0, 0, 0, 0), pipeline_mode=pl.Buffered(1)
+            ),
+        ],
+        out_specs=[
+            pl.BlockSpec((group, width), lambda i: (i, 0)),
+            pl.BlockSpec((group, width), lambda i: (i, 0)),
+            pl.BlockSpec(slots.shape, whole),
+            pl.BlockSpec(memory_space=pltpu.HBM),
+        ],
+        scratch_shapes=[
+            pltpu.VMEM((held, width), jnp.bfloat16),
+            pltpu.VMEM((held, width), jnp.bfloat16),
+            pltpu.VMEM((held, width), jnp.bfloat16),
+            pltpu.VMEM((three, width, ff), jnp.float32),
+            pltpu.SemaphoreType.DMA,
+        ],
+        compiler_params=pltpu.CompilerParams(vmem_limit_bytes=63 << 20),
+        name="run_expert",
+    )(slots, gates, tokens, upstream, weights)
+
+
+def split_body(
+    block_in,
+    segments,
+    routes,
+    attn_gain,
+    query_key_value_weight,
+    q_gain,
+    k_gain,
+    w_out,
+    ffn_gain,
+    router,
+    expert_weights,
+    cotangent,
+):
+    tok, width = block_in.shape
+    seq = segments.shape[0]
+    experts = router.shape[1]
+    capacity = tok * routes.shape[1] * 2 // experts
+    heads = QUERY_HEADS // 4
+    both = ("rep", "shard")
+    upstream_all = lax.all_gather(cotangent, both, axis=0, tiled=True)
+    x_all, weight = start_exchange(block_in, query_key_value_weight, 0)
+
+    mask = jnp.any(
+        routes[:, :, None] == jnp.arange(experts, dtype=jnp.int32)[None, None, :], axis=1
+    )
+    mask_f = mask.astype(jnp.float32)
+    earlier = (jnp.arange(tok)[:, None] > jnp.arange(tok)[None, :]).astype(jnp.bfloat16)
+    slot = jnp.dot(earlier, mask.astype(jnp.bfloat16), preferred_element_type=jnp.float32)
+    slot_table = jnp.where(mask, slot, -4096.0).T
+
+    inputs_all = x_all.astype(jnp.float32)
+    normed_one = (inputs_all * rms_scale(inputs_all) * attn_gain).astype(jnp.bfloat16)
+    query_key_value = jnp.dot(normed_one, weight, preferred_element_type=jnp.float32)
+    q_raw = query_key_value[:, : heads * HEAD_SIZE].reshape(seq, heads, HEAD_SIZE)
+    k_raw = query_key_value[:, heads * HEAD_SIZE : (heads + 1) * HEAD_SIZE].reshape(
+        seq, 1, HEAD_SIZE
+    )
+    values = query_key_value[:, (heads + 1) * HEAD_SIZE :].reshape(seq, 1, HEAD_SIZE)
+    values = values.astype(jnp.bfloat16)
+    positions = jnp.arange(seq, dtype=jnp.int32)
+    cosine, sine = rope_tables(positions)
+    q_scale, q_rot = norm_rope(q_raw, q_gain, cosine, sine)
+    k_scale, k_rot = norm_rope(k_raw, k_gain, cosine, sine)
+    allowed = (segments[:, None] == segments[None, :]) & (positions[None, :] <= positions[:, None])
+    attended_f, lse = attend_forward(q_rot, k_rot, values, allowed)
+    attended = attended_f.astype(jnp.bfloat16)
+    partial = jnp.dot(attended, w_out, preferred_element_type=jnp.float32).astype(jnp.bfloat16)
+    inputs = block_in.astype(jnp.float32)
+    middle = inputs + fold_sequence(partial, 1)
+    scale_two = rms_scale(middle)
+    normed_two = (middle * scale_two * ffn_gain).astype(jnp.bfloat16)
+    logits = jnp.dot(normed_two, router, preferred_element_type=jnp.float32)
+    weights = jax.nn.softmax(logits, axis=-1)
+    picked = weights * mask_f
+    total = jnp.sum(picked, axis=1, keepdims=True)
+    gates = picked / total
+    table = jnp.concatenate([gates.T, slot_table], axis=0)
+    tokens_all, table_all = gather_all([normed_two, table], 2)
+    expert = lax.axis_index(both)
+    table_all = table_all.reshape(-1, 2, experts, tok)
+    own = lax.dynamic_index_in_dim(table_all, expert, 2, keepdims=False)
+    out_part, grad_part, gate_part, grad_experts = run_expert(
+        own[:, 1], own[:, 0], tokens_all, upstream_all, expert_weights, capacity
+    )
+    grad_gates = lax.all_to_all(gate_part, both, split_axis=0, concat_axis=0, tiled=True).T
+    grad_from_experts = reduce_all(grad_part, 3).astype(jnp.float32)
+    expert_sum = reduce_all(out_part, 4).astype(jnp.float32)
+    block_out = (middle + expert_sum).astype(jnp.bfloat16)
+
+    upstream = cotangent.astype(jnp.float32)
+    grad_picked = grad_gates / total - jnp.sum(grad_gates * picked, axis=1, keepdims=True) / (
+        total * total
+    )
+    grad_weights = grad_picked * mask_f
+    grad_logits = weights * (grad_weights - jnp.sum(grad_weights * weights, axis=1, keepdims=True))
+    grad_from_router = jnp.dot(
+        grad_logits, router.astype(jnp.float32).T, precision=lax.Precision.HIGHEST
+    )
+    grad_router = jnp.dot(
+        normed_two.astype(jnp.float32).T, grad_logits, precision=lax.Precision.HIGHEST
+    )
+    grad_norm_two, grad_ffn_gain = rms_back(
+        middle, scale_two, ffn_gain, grad_from_experts + grad_from_router
+    )
+    grad_middle = upstream + grad_norm_two
+    grad_middle_all = spread_sequence(grad_middle.astype(jnp.bfloat16), 5)
+    grad_out = lax.dot_general(
+        attended, grad_middle_all, (((0,), (0,)), ((), ())), preferred_element_type=jnp.float32
+    ).astype(jnp.bfloat16)
+    grad_out = lax.psum(grad_out, "rep").astype(jnp.float32)
+    grad_attended = jnp.dot(
+        grad_middle_all, w_out.T, preferred_element_type=jnp.float32
+    ).astype(jnp.bfloat16)
+    grad_q_rot, grad_k_rot, grad_v = attend_backward(
+        q_rot, k_rot, values, allowed, lse, attended, grad_attended
+    )
+    grad_q_raw, grad_q_gain = norm_rope_back(q_raw, q_scale, q_gain, cosine, sine, grad_q_rot)
+    grad_k_raw, grad_k_gain = norm_rope_back(k_raw, k_scale, k_gain, cosine, sine, grad_k_rot)
+    grad_qkv_b = jnp.concatenate(
+        [grad_q_raw.reshape(seq, -1), grad_k_raw.reshape(seq, -1), grad_v.reshape(seq, -1)], axis=1
+    ).astype(jnp.bfloat16)
+    grad_norm_one = fold_sequence(
+        jnp.dot(grad_qkv_b, weight.T, preferred_element_type=jnp.float32).astype(jnp.bfloat16), 6
+    )
+    grad_weight = lax.dot_general(
+        normed_one, grad_qkv_b, (((0,), (0,)), ((), ())), preferred_element_type=jnp.float32
+    ).astype(jnp.bfloat16)
+    grad_weight = lax.all_to_all(
+        grad_weight.reshape(4, -1, grad_weight.shape[1]), "shard", split_axis=0, concat_axis=0, tiled=True
+    )
+    grad_weight = lax.psum(grad_weight, "rep").astype(jnp.float32)
+    cut = heads * HEAD_SIZE
+    depth = grad_weight.shape[1]
+    grad_qkv = jnp.concatenate(
+        [
+            grad_weight[:, :, low:high].transpose(1, 0, 2).reshape(depth, -1)
+            for low, high in ((0, cut), (cut, cut + HEAD_SIZE), (cut + HEAD_SIZE, cut + 2 * HEAD_SIZE))
+        ],
+        axis=1,
+    )
+    grad_inputs, grad_attn_gain = rms_back(inputs, rms_scale(inputs), attn_gain, grad_norm_one)
+    grad_input = (grad_middle + grad_inputs).astype(jnp.bfloat16)
+    grad_attn_gain, grad_q_gain, grad_k_gain, grad_ffn_gain, grad_router = lax.psum(
+        (grad_attn_gain, grad_q_gain, grad_k_gain, grad_ffn_gain, grad_router), both
+    )
+    return (
+        block_out,
+        grad_input,
+        grad_attn_gain,
+        grad_qkv,
+        grad_q_gain,
+        grad_k_gain,
+        grad_out,
+        grad_ffn_gain,
+        grad_router,
+        grad_experts,
+    )
+
+
 def solution(mesh):
     placed = (
         P(("rep", "shard"), None),
@@ -365,6 +1273,7 @@
         P(("rep", "shard"), None, None, None),
         P(("rep", "shard"), None),
     )
+    body = split_body if dict(mesh.shape) == {"rep": 8, "shard": 4} else plain_body
     return jax.shard_map(
         body,
         mesh=mesh,

time: 2370 us -> 1010 us (0.43)
  waiting for transfers between devices: 1210 us -> 288 us
  Pallas kernels: 0 us -> 509 us
  blocking collectives: 441 us -> 53.9 us
  local copies, waits for them, and re-layouts: 274 us -> 38.4 us
  other arithmetic: 207 us -> 39 us
  matrix products: 209 us -> 48.2 us
    pallas_call x0 -> x8, Pallas kernels: none -> 509 us  [the longest x2 187 us: reduce_all(): pl.pallas_call(reduce_kernel, out_shape=jax.ShapeDtypeStruct((rows, width...]
    all_to_all x1 -> x0, blocking collectives: 369 us -> none  [body(): lax.all_to_all(buffer, ('rep', 'shard'), split_axis=0, concat_axis=1, til...]
    all_to_all x1 -> x2, waiting for transfers between devices: 382 us -> 52.7 us  [the longest x1 52.7 us: split_body(): lax.all_to_all(grad_weight.reshape(4, -1, grad_weight.shape[1]), 'shard',...]
    reduce_scatter x4 -> x0, waiting for transfers between devices: 327 us -> none  [the longest x1 191 us: body(): lax.psum_scatter(lax.dot_general(columns, grad_qkv_b, (((0,), (0,)), ((),...]
    all_gather x2 -> x1, waiting for transfers between devices: 271 us -> 0.01 us  [split_body(): upstream_all = lax.all_gather(cotangent, both, axis=0, tiled=True)]
    dot_general x37 -> x6, matrix products: 143 us -> 19.4 us  [product(): return jnp.einsum(form, left, right, preferred_element_type=jnp.float32)]
    unnamed x4 -> x1, other arithmetic: 103 us -> 0.01 us
    unnamed x205 -> x150, local copies, waits for them, and re-layouts: 105 us -> 19.7 us
  transfers between devices with their start and end apart: 9 -> 5, of which waited for: 8 -> 3; matrix products, arithmetic and copies ran while one was open for 8% -> 7% of each run, Pallas kernels for 0% -> 39%
where the time goes in v1:
time: 1010 us; the launch traced here: 1000 us
  Pallas kernels  509 us (50%)
  waiting for transfers between devices  288 us (29%)
  blocking collectives  53.9 us (5%)
  matrix products  48.2 us (5%)
  other arithmetic  39 us (4%)
  local copies, waits for them, and re-layouts  38.4 us (4%)
  between operations  15.1 us (1%)
    pallas_call x2, Pallas kernels, reduce_all(): pl.pallas_call(reduce_kernel, out_shape=jax.ShapeDtypeStruct((rows, width...  187 us
    psum x1, waiting for transfers between devices, split_body(): grad_weight = lax.psum(grad_weight, 'rep').astype(jnp.float32)  118 us
    psum x1, waiting for transfers between devices, split_body(): lax.psum((grad_attn_gain, grad_q_gain, grad_k_gain, grad_ffn_gain, grad_r...  116 us
    pallas_call x1, Pallas kernels, run_expert(): pl.pallas_call(expert_kernel, grid=(steps,), out_shape=[jax.ShapeDtypeStr...  89.9 us
    pallas_call x1, Pallas kernels, gather_all(): pl.pallas_call(functools.partial(gather_kernel, rows), out_shape=[jax.Sha...  79.3 us
    pallas_call x1, Pallas kernels, start_exchange(): pl.pallas_call(start_kernel, out_shape=[jax.ShapeDtypeStruct((tok * 4, wi...  74.9 us
    psum x1, blocking collectives, split_body(): lax.psum((grad_attn_gain, grad_q_gain, grad_k_gain, grad_ffn_gain, grad_r...  53.9 us
    all_to_all x1, waiting for transfers between devices, split_body(): lax.all_to_all(grad_weight.reshape(4, -1, grad_weight.shape[1]), 'shard',...  52.7 us
  transfers between devices with their start and end apart: 5, of which 3 were waited for; matrix products, arithmetic and copies ran while one was open for 7% of the time, Pallas kernels for 39%

profile of v1, /device:TPU:0, one launch (start us, length us, event | category | flops | bytes accessed | tf_op | source)
XLA Modules:
  0.0 1000.2 jit_solution(1446428163256627593)
XLA Ops:
  9.0 2.5 copy-done.5
  11.5 74.9 %start_exchange.1 = (bf16[512,2048]{1,0:T(8,128)(2,1)S(1)}, bf16[2048,1280]{1,0:T(8,128)(2,1)S(1)}) custom-call(bf16[128,2048]{1,0:T(8,128)(2,1)S(1)} %copy-done.2, bf16[512,5120]{1,0:T(8,128)(2,1)S(1)} %copy-done.5), custom_call_target="tpu_custom_call" | custom-call | tf_op jit(solution)/shard_map/start_exchange/pallas_call | solution.py:867
  87.8 2.9 fusion.24
  95.0 1.8 copy.184
  96.8 1.9 copy.141
  98.7 3.0 multiply_reduce_fusion.3
  103.9 2.1 copy.175
  106.1 1.6 mul.495
  107.7 2.9 copy.174
  110.7 1.6 mul.488
  112.2 3.2 copy.173
  115.7 5.1 fusion.4
  120.8 1.8 exponential_reduce_fusion
  122.6 1.6 copy-done.11
  124.2 2.5 convolution_convert_fusion.4
  127.8 2.4 convolution_convert_fusion.2.part_ref
  130.2 25.9 %fold_sequence.2 = f32[128,2048]{1,0:T(8,128)S(1)} custom-call(bf16[512,2048]{1,0:T(8,128)(2,1)S(1)} %convolution_convert_fusion.2.part_ref), custom_call_target="tpu_custom_call" | custom-call | tf_op jit(solution)/shard_map/fold_sequence/pallas_call | solution.py:971
  158.3 79.3 %gather_all.1 = (bf16[4096,2048]{1,0:T(8,128)(2,1)}, f32[2048,128]{1,0:T(8,128)S(1)}) custom-call(bf16[128,2048]{1,0:T(8,128)(2,1)S(1)} %multiply_convert_fusion.refs_0_, f32[64,128]{1,0:T(8,128)S(1)} %pad_maximum_fusion.6.refs_1_), custom_call_target="tpu_custom_call" | custom-call | tf_op jit(solution)/shard_map/gather_all/pallas_call | solution.py:545
  238.4 89.9 %run_expert.1 = (bf16[4096,2048]{1,0:T(8,128)(2,1)}, bf16[4096,2048]{1,0:T(8,128)(2,1)}, f32[32,128]{1,0:T(8,128)}, f32[1,3,2048,768]{3,2,1,0:T(8,128)}) custom-call(f32[32,128]{1,0:T(8,128)} %get-tuple-element.116.slots_ref, f32[32,128]{1,0:T(8,128)} %get-tuple-element.115.gates_ref, bf16[4096,2048]{1,0:T(8,128)(2,1)} %get-tuple-element.75.x_ref, ...), custom_call_target="tpu_custom_call" | custom-call | tf_op jit(solution)/shard_map/run_expert/pallas_call | solution.py:1085
  328.3 4.1 all-to-all-start
  332.4 87.7 %reduce_all.3 = bf16[128,2048]{1,0:T(8,128)(2,1)} custom-call(bf16[4096,2048]{1,0:T(8,128)(2,1)} %get-tuple-element.77.part_ref), custom_call_target="tpu_custom_call" | custom-call | tf_op jit(solution)/shard_map/reduce_all/pallas_call | solution.py:730
  420.1 99.4 %reduce_all.2 = bf16[128,2048]{1,0:T(8,128)(2,1)} custom-call(bf16[4096,2048]{1,0:T(8,128)(2,1)} %get-tuple-element.76.part_ref), custom_call_target="tpu_custom_call" | custom-call | tf_op jit(solution)/shard_map/reduce_all/pallas_call | solution.py:730
  519.8 2.1 multiply_reduce_fusion.4
  521.9 1.6 fusion.49
  523.5 26.2 %spread_sequence.1 = bf16[512,2048]{1,0:T(8,128)(2,1)S(1)} custom-call(bf16[128,2048]{1,0:T(8,128)(2,1)S(1)} %get-tuple-element.96.x_ref), custom_call_target="tpu_custom_call" | custom-call | tf_op jit(solution)/shard_map/spread_sequence/pallas_call | solution.py:917
  549.6 3.3 convolution_convert_fusion.5
  553.0 2.3 copy.149
  555.3 1.8 multiply_reduce_fusion.2
  557.2 6.8 fusion.2
  567.6 1.4 slice-done.1
  569.1 3.0 fusion.8
  573.7 1.9 multiply_reduce_fusion
  578.6 3.0 subtract_convert_fusion
  581.7 5.3 convolution_convert_fusion
  587.0 5.1 all-to-all-start.1
  592.1 5.6 convolution_convert_fusion.1
  597.8 52.7 %all-to-all-done.1 = bf16[4,512,1280]{2,1,0:T(8,128)(2,1)} async-done(((bf16[4,512,1280]{2,1,0:T(8,128)(2,1)}), bf16[4,512,1280]{2,1,0:T(8,128)(2,1)}, u32[]{:S(2)}, u32[]{:S(2)}) %all-to-all-start.1) | async-done | bytes 5242912 | tf_op jit(solution)/shard_map/all_to_all | solution.py:1229
  651.7 5.7 convolution_convert_fusion.3.part_ref
  657.4 25.4 %fold_sequence.3 = f32[128,2048]{1,0:T(8,128)S(1)} custom-call(bf16[512,2048]{1,0:T(8,128)(2,1)S(1)} %convolution_convert_fusion.3.part_ref), custom_call_target="tpu_custom_call" | custom-call | tf_op jit(solution)/shard_map/fold_sequence/pallas_call | solution.py:971
  684.2 2.5 fusion.13
  686.8 53.9 %all-reduce = (f32[2048]{0:T(1024)}, f32[128]{0:T(128)}, f32[128]{0:T(128)}, f32[2048]{0:T(1024)}) all-reduce(f32[2048]{0:T(1024)S(1)} %get-tuple-element.86, f32[128]{0:T(128)S(1)} %get-tuple-element.80, f32[128]{0:T(128)S(1)} %get-tuple-element.82, f32[2048]{0:T(1024)S(1)} %get-tuple-element.84), channel_id=1, replica_groups=mesh['rep'=8,'shard'=4] {'rep','shard'}, use_global_device_ids=true, to_apply=%region_19.20 | all-reduce | flops 4352 | bytes 34816 | tf_op jit(solution)/shard_map/psum | solution.py:1244
  740.7 118.3 %all-reduce.7.cloned.1.call-done = (bf16[4,512,1280]{2,1,0:T(8,128)(2,1)}, bf16[1024,2048]{1,0:T(8,128)(2,1)}) async-done(((bf16[4,512,1280]{2,1,0:T(8,128)(2,1)}, bf16[1024,2048]{1,0:T(8,128)(2,1)}), (bf16[4,512,1280]{2,1,0:T(8,128)(2,1)}, bf16[1024,2048]{1,0:T(8,128)(2,1)})) %all-reduce.7.cloned.1.call-update) | async-done | bytes 9437200 | tf_op jit(solution)/shard_map/psum | solution.py:1232
  859.0 3.4 convert_element_type.154
  863.9 1.7 copy.181
  865.8 5.6 pad_maximum_fusion
  871.5 4.4 convert_element_type.156
  875.9 115.9 %all-reduce.5.cloned.1.call-done = f32[2048,32]{0,1:T(8,128)} async-done(((f32[2048,32]{0,1:T(8,128)}), f32[2048,32]{0,1:T(8,128)}) %all-reduce.5.cloned.1.call-update) | async-done | bytes 262160 | tf_op jit(solution)/shard_map/psum | solution.py:1244
  991.8 1.7 copy.198
  (205 shorter events, 26.5 us)
Async XLA Ops:
  7.2 150.4 %copy-start = (bf16[2048,32]{0,1:T(8,128)(2,1)S(1)}, bf16[2048,32]{0,1:T(8,128)(2,1)}, u32[]{:S(2)}) copy-start(bf16[2048,32]{0,1:T(8,128)(2,1)} %param.21) | copy-start | bytes 393220
  7.2 231.1 %all-gather.2.cloned.1.call-start = ((), (), s32[]{:S(2)}) async-start(), calls=%async_computation.2 | async-start | bytes 17301504 | tf_op jit(solution)/shard_map/all_gather | solution.py:1141
  11.5 76.4 %copy-start.39 = (f32[2048]{0:T(1024)S(1)}, f32[2048]{0:T(1024)}, u32[]{:S(2)}) copy-start(f32[2048]{0:T(1024)} %param.15) | copy-start | bytes 24580
  86.3 4.4 copy-start.6
  86.3 4.4 copy-start.8
  87.8 3.9 copy-start.52
  90.8 4.2 copy-start.18
  94.6 21.1 %copy-start.32 = (bf16[512,128]{1,0:T(8,128)(2,1)}, bf16[512,128]{1,0:T(8,128)(2,1)S(1)}, u32[]{:S(2)}) copy-start(bf16[512,128]{1,0:T(8,128)(2,1)S(1)} %get-tuple-element.110) | copy-start | bytes 393220
  94.7 8.9 copy-start.26
  96.8 5.1 copy-start.54
  98.7 3.6 copy-start.9
  103.9 3.8 copy-start.14
  112.2 3.2 copy-start.50
  112.2 3.5 copy-start.19
  115.7 6.9 copy-start.22
  120.8 3.4 copy-start.11
  124.2 3.6 copy-start.67
  130.2 25.9 %copy-start.3 = (bf16[128,2048]{1,0:T(8,128)(2,1)S(1)}, bf16[128,2048]{1,0:T(8,128)(2,1)}, u32[]{:S(2)}) copy-start(bf16[128,2048]{1,0:T(8,128)(2,1)} %x_ref.1) | copy-start | bytes 1572868
  130.2 27.3 %copy-start.38 = (f32[2048]{0:T(1024)S(1)}, f32[2048]{0:T(1024)}, u32[]{:S(2)}) copy-start(f32[2048]{0:T(1024)} %param.20) | copy-start | bytes 24580
  157.9 80.4 %copy-start.41 = (f32[128]{0:T(128)}, f32[128]{0:T(128)S(1)}, u32[]{:S(2)}) copy-start(f32[128]{0:T(128)S(1)} %get-tuple-element.129) | copy-start | bytes 1540
  158.0 80.3 %copy-start.43 = (f32[128]{0:T(128)}, f32[128]{0:T(128)S(1)}, u32[]{:S(2)}) copy-start(f32[128]{0:T(128)S(1)} %fusion.40) | copy-start | bytes 1540
  158.1 80.2 %copy-start.47 = (f32[128]{0:T(128)}, f32[128]{0:T(128)S(1)}, u32[]{:S(2)}) copy-start(f32[128]{0:T(128)S(1)} %fusion.41) | copy-start | bytes 1540
  328.3 191.3 %all-to-all-start = ((f32[32,1,128]{2,1,0:T(1,128)}), f32[32,1,128]{2,1,0:T(1,128)S(1)}, u32[]{:S(2)}, u32[]{:S(2)}) async-start(f32[32,1,128]{2,1,0:T(1,128)} %bitcast.161), calls=%async_computation | async-start | bytes 32768 | tf_op jit(solution)/shard_map/all_to_all | solution.py:1186
  420.1 99.5 %copy-start.42 = (f32[128]{0:T(128)S(1)}, f32[128]{0:T(128)}, u32[]{:S(2)}) copy-start(f32[128]{0:T(128)} %copy-done.41) | copy-start | bytes 1540
  420.1 99.5 %copy-start.44 = (f32[128]{0:T(128)S(1)}, f32[128]{0:T(128)}, u32[]{:S(2)}) copy-start(f32[128]{0:T(128)} %copy-done.43) | copy-start | bytes 1540
  420.1 99.6 %copy-start.48 = (f32[128]{0:T(128)S(1)}, f32[128]{0:T(128)}, u32[]{:S(2)}) copy-start(f32[128]{0:T(128)} %copy-done.47) | copy-start | bytes 1540
  420.1 99.6 %copy-start.17 = (f32[128,2048]{1,0:T(8,128)S(1)}, f32[128,2048]{1,0:T(8,128)}, u32[]{:S(2)}) copy-start(f32[128,2048]{1,0:T(8,128)} %copy-done.16) | copy-start | bytes 3145732
  420.1 99.6 %copy-start.57 = (f32[128]{0:T(128)S(1)}, f32[128]{0:T(128)}, u32[]{:S(2)}) copy-start(f32[128]{0:T(128)} %copy-done.56) | copy-start | bytes 1540
  519.7 3.8 copy-start.58
  519.8 3.7 copy-start.60
  521.9 27.8 %copy-start.68 = (bf16[1024,2048]{1,0:T(8,128)(2,1)S(1)}, bf16[1024,2048]{1,0:T(8,128)(2,1)}, u32[]{:S(2)}) copy-start(bf16[1024,2048]{1,0:T(8,128)(2,1)} %param.19) | copy-start | bytes 12582916
  553.0 4.2 copy-start.23
  553.0 4.2 copy-start.46
  557.2 6.8 copy-start.27
  557.2 6.8 copy-start.33
  564.1 3.5 slice-start
  578.6 3.1 copy-start.7
  578.6 3.1 copy-start.40
  581.6 5.4 copy-start.36
  587.0 63.4 %all-to-all-start.1 = ((bf16[4,512,1280]{2,1,0:T(8,128)(2,1)}), bf16[4,512,1280]{2,1,0:T(8,128)(2,1)}, u32[]{:S(2)}, u32[]{:S(2)}) async-start(bf16[4,512,1280]{2,1,0:T(8,128)(2,1)} %bitcast.148), calls=%async_computation.1 | async-start | bytes 10485760 | tf_op jit(solution)/shard_map/all_to_all | solution.py:1229
  592.1 266.9 %all-reduce.7.cloned.1.call-start = ((), (), s32[]{:S(2)}) async-start(), calls=%async_computation.4 | async-start | bytes 18874368 | tf_op jit(solution)/shard_map/psum | solution.py:1232
  650.5 341.3 %all-reduce.5.cloned.1.call-start = ((), (), s32[]{:S(2)}) async-start(), calls=%async_computation.3 | async-start | bytes 524288 | tf_op jit(solution)/shard_map/psum | solution.py:1244
  657.3 25.5 %copy-start.4 = (bf16[128,2048]{1,0:T(8,128)(2,1)S(1)}, bf16[128,2048]{1,0:T(8,128)(2,1)}, u32[]{:S(2)}) copy-start(bf16[128,2048]{1,0:T(8,128)(2,1)} %x_ref.1) | copy-start | bytes 1572868
  657.4 25.8 %copy-start.49 = (f32[128]{0:T(128)S(1)}, f32[128]{0:T(128)}, u32[]{:S(2)}) copy-start(f32[128]{0:T(128)} %copy-done.47) | copy-start | bytes 1540
  657.4 25.8 %copy-start.59 = (f32[128]{0:T(128)S(1)}, f32[128]{0:T(128)}, u32[]{:S(2)}) copy-start(f32[128]{0:T(128)} %copy-done.58) | copy-start | bytes 1540
  657.4 25.8 %copy-start.61 = (f32[128]{0:T(128)S(1)}, f32[128]{0:T(128)}, u32[]{:S(2)}) copy-start(f32[128]{0:T(128)} %copy-done.60) | copy-start | bytes 1540
  865.8 5.6 copy-start.20
  871.5 122.0 %copy-start.1 = (bf16[2048,32]{0,1:T(8,128)(2,1)S(1)}, bf16[2048,32]{0,1:T(8,128)(2,1)}, u32[]{:S(2)}) copy-start(bf16[2048,32]{0,1:T(8,128)(2,1)} %param.21) | copy-start | bytes 393220
  (29 other events, 53.1 us)
Sparse Core Ops, SparseCore 0:
  10.9 135.1 all-gather.1
  650.6 208.3 all-reduce.6
  865.1 126.6 all-reduce.4
